TPU v7x, 128 devices: a whole 4x4x4 slice. The times are simulated.
128 devices in a mesh: dp: 32 (over x, z, core), mp: 4 (over y).
Axes of the slice: x: 4, y: 4, z: 4, core: 2. Of those that a mesh axis runs over, the one named last changes fastest.
Arguments:
- acts: bfloat16 [1, 65536, 4096], P(None, 'dp'), may hold values from -64 to 64
- out_grads: bfloat16 [1, 65536, 4096], P(None, 'dp', 'mp'), may hold values from -80 to 80
- clip_bound: float32 [1], replicated, may hold values from 163840 to 491520
- noise: float32 [1, 4096, 4096], P(None, 'dp', 'mp'), may hold values from -6 to 6
Outputs:
- update: float32 [1, 4096, 4096], P(None, 'dp', 'mp')
All inputs are finite; a program needn't handle non-finite values.
Results may differ from a plain program's by a relative error of at most 0.0017.
Values may be sent and summed in bfloat16 or wider, within the bound.
A program may use at most 128 MiB of HBM per device.

v0:
```python
import math

import jax
import jax.numpy as jnp
from jax import lax
from jax.sharding import PartitionSpec as P

SEQ = 512


def sent_to_all(array, axis):
    devices = lax.axis_size(axis)
    return lax.all_to_all(
        jnp.broadcast_to(array[None], (devices, *array.shape)), axis, 0, 0, tiled=True
    )


def over_copies(array, axis):
    everything = sent_to_all(array, axis)
    return jnp.sum(everything, axis=0)


def ghost_partial(act_block, grad_block, examples):
    act_seq = act_block.reshape(examples, SEQ, act_block.shape[1])
    grad_seq = grad_block.reshape(examples, SEQ, grad_block.shape[1])
    gram_act = jnp.einsum("etd,esd->ets", act_seq, act_seq, preferred_element_type=jnp.float32)
    gram_grad = jnp.einsum("etd,esd->ets", grad_seq, grad_seq, preferred_element_type=jnp.float32)
    return jnp.sum(gram_act * gram_grad, axis=(1, 2))


def scale_grads(grad_block, norm_sq, bound, examples):
    clip = jnp.minimum(1.0, bound / jnp.sqrt(norm_sq + 1e-06))
    factor = clip / bound
    grad_seq = grad_block.reshape(examples, SEQ, grad_block.shape[1]).astype(jnp.float32)
    scaled = (grad_seq * factor[:, None, None]).astype(jnp.bfloat16)
    return scaled.reshape(grad_block.shape)


def on_device(acts, out_grads, clip_bound, noise):
    examples = acts.shape[1] // SEQ
    model_width = acts.shape[2]
    batch_total = examples * lax.axis_size("dp")
    out_factor = model_width / math.sqrt(batch_total)
    act_block = acts[0]
    norm_sq = over_copies(ghost_partial(act_block, out_grads[0], examples), "mp")
    scaled = scale_grads(out_grads[0], norm_sq, clip_bound[0], examples)

    def term_rows(begin_row, row_count, act_block=act_block, scaled=scaled):
        return lax.dot_general(
            act_block, scaled, (((0,), (0,)), ((), ())), preferred_element_type=jnp.float32
        )

    summed = lax.psum_scatter(
        term_rows(jnp.int32(0), model_width // lax.axis_size("dp") * lax.axis_size("dp")),
        "dp",
        scatter_dimension=0,
        tiled=True,
    )
    updates = [summed * out_factor + noise[0]]
    return jnp.stack(updates)


def solution(mesh):
    placed = (P(None, "dp", None), P(None, "dp", "mp"), P(), P(None, "dp", "mp"))
    return jax.shard_map(
        on_device, mesh=mesh, in_specs=placed, out_specs=P(None, "dp", "mp"), check_vma=False
    )
```

profile of v0, /device:TPU:0, one launch (start us, length us, event | category | flops | bytes accessed | tf_op | source)
XLA Modules:
  0.0 190.8 jit_solution(14214695495248306600)
XLA Ops:
  6.5 7.8 %fusion.9 = f32[4,512,512]{2,1,0:T(8,128)} fusion(bf16[4,512,1024]{2,1,0:T(8,128)(2,1)} %bitcast.31), kind=kOutput, calls=%fused_computation.11 | convolution fusion | flops 2147483648 | bytes 8388608 | tf_op jit(solution)/shard_map/etd,esd->ets/dot_general | solution.py:27
  14.3 16.9 %multiply_reduce_fusion = f32[4]{0:T(128)S(1)} fusion(f32[4,512,512]{2,1,0:T(8,128)} %fusion.9, bf16[4,512,4096]{2,1,0:T(8,128)(2,1)} %bitcast.30), kind=kOutput, calls=%fused_computation.6 | convolution fusion | flops 8592031744 | bytes 20971536 | tf_op jit(solution)/shard_map/etd,esd->ets/dot_general | solution.py:26
  31.2 0.6 broadcast_in_dim.2
  31.8 4.6 %all-to-all-start = ((f32[4,1,4]{2,1,0:T(1,128)}), f32[4,1,4]{2,1,0:T(1,128)S(1)}, u32[]{:S(2)}, u32[]{:S(2)}) async-start(f32[4,1,4]{2,1,0:T(1,128)} %broadcast_in_dim.2), calls=%async_computation | async-start | bytes 4096 | tf_op jit(solution)/shard_map/all_to_all | solution.py:13
  36.3 0.0 reduce-scatter.2.cloned.1.call-start
  37.0 4.6 %all-to-all-done = f32[4,1,4]{2,1,0:T(1,128)S(1)} async-done(((f32[4,1,4]{2,1,0:T(1,128)}), f32[4,1,4]{2,1,0:T(1,128)S(1)}, u32[]{:S(2)}, u32[]{:S(2)}) %all-to-all-start) | async-done | bytes 96 | tf_op jit(solution)/shard_map/all_to_all | solution.py:13
  41.6 0.1 broadcast_bitcast_fusion
  41.7 24.2 %fusion.2 = f32[4096,1024]{0,1:T(8,128)} fusion(bf16[1,2048,4096]{2,1,0:T(8,128)(2,1)} %param.4, bf16[1,2048,1024]{2,1,0:T(8,128)(2,1)} %param.5, f32[2048]{0:T(1024)S(1)} %bitcast.28), kind=kOutput, calls=%fused_computation.2 | convolution fusion | flops 17186160640 | bytes 37756928 | tf_op jit(solution)/shard_map/dot_general | solution.py:49
  65.9 0.0 copy-start
  65.9 0.0 reduce-scatter.2.cloned.1.call-update
  65.9 1.0 copy-done
  66.9 0.2 copy.10
  67.1 114.7 %reduce-scatter.2.cloned.1.call-done = f32[128,1024]{0,1:T(8,128)} async-done(((f32[4096,1024]{0,1:T(8,128)}), f32[128,1024]{0,1:T(8,128)}) %reduce-scatter.2.cloned.1.call-update) | async-done | bytes 524304 | tf_op jit(solution)/shard_map/reduce_scatter | solution.py:53
  181.9 1.1 fusion.8
  183.0 1.0 copy.11
  (3 shorter events, 0.0 us)
Async XLA Ops:
  31.8 9.8 %all-to-all-start = ((f32[4,1,4]{2,1,0:T(1,128)}), f32[4,1,4]{2,1,0:T(1,128)S(1)}, u32[]{:S(2)}, u32[]{:S(2)}) async-start(f32[4,1,4]{2,1,0:T(1,128)} %broadcast_in_dim.2), calls=%async_computation | async-start | bytes 4096 | tf_op jit(solution)/shard_map/all_to_all | solution.py:13
  36.3 145.5 %reduce-scatter.2.cloned.1.call-start = ((), (), s32[]{:S(2)}) async-start(), calls=%async_computation.2 | async-start | bytes 17301504 | tf_op jit(solution)/shard_map/reduce_scatter | solution.py:53
  65.9 1.0 copy-start
Sparse Core Ops, SparseCore 0:
  66.0 115.7 reduce-scatter.1
where the time goes:
time: 191 us
  waiting for transfers between devices  119 us (62%)
  matrix products  48.9 us (26%)
  between operations  14.1 us (7%)
  starting transfers between devices  4.58 us (2%)
  local copies, waits for them, and re-layouts  2.87 us (2%)
    reduce_scatter x1, waiting for transfers between devices, on_device(): lax.psum_scatter(term_rows(jnp.int32(0), model_width // lax.axis_size('dp...  115 us
    dot_general x1, matrix products, term_rows(): lax.dot_general(act_block, scaled, (((0,), (0,)), ((), ())), preferred_el...  24.2 us
    dot_general x1, matrix products, ghost_partial(): jnp.einsum('etd,esd->ets', act_seq, act_seq, preferred_element_type=jnp.f...  16.9 us
    dot_general x1, matrix products, ghost_partial(): jnp.einsum('etd,esd->ets', grad_seq, grad_seq, preferred_element_type=jnp...  7.76 us
    all_to_all x1, starting transfers between devices, sent_to_all(): lax.all_to_all(jnp.broadcast_to(array[None], (devices, *array.shape)), ax...  4.57 us
    all_to_all x1, waiting for transfers between devices, sent_to_all(): lax.all_to_all(jnp.broadcast_to(array[None], (devices, *array.shape)), ax...  4.55 us
  transfers between devices with their start and end apart: 2, of which 2 were waited for; matrix products, arithmetic and copies ran while one was open for 0% of the time, Pallas kernels for 0%

commit v1 on v0

v1 whole, which is shorter than its diff:
```python
import math

import jax
import jax.numpy as jnp
from jax import lax
from jax.experimental import pallas as pl
from jax.experimental.pallas import tpu as pltpu
from jax.sharding import PartitionSpec as P

SEQ = 512
RING = 4
MESH = pl.DeviceIdType.MESH
F32 = jnp.float32
BF16 = jnp.bfloat16
CONTRACT_LAST = (((1,), (1,)), ((), ()))


def fold(product):
    rows, cols = product.shape
    return jnp.sum(product.reshape(rows // 8, 8, cols // 128, 128), axis=(0, 2))


def kernel(acts, grads, bound, out, abuf, graw, acts_c, g_t, norm_own, norm_all,
           s_opp, s_nb, hold, r_opp, r_fin, own, r2_opp, s2, r2_fin,
           abuf_sem, grad_sem, col_sem, xs_acts, xr_acts, xs_grads, xr_grads, ns_sem, nr_sem,
           s1_opp, r1_opp, s1_fin, r1_fin, s2_opp, r2o_sem, s2_fin, r2f_sem):
    dp = lax.axis_index("dp")
    y = lax.axis_index("mp")
    x, z, c = dp // (2 * RING), (dp // 2) % RING, dp % 2
    tokens = acts.shape[0]
    examples = tokens // SEQ
    blocks = acts.shape[1] // 256
    half_cols = grads.shape[1] // 2

    def at(xx, zz, cc=c, yy=y):
        return ((xx % RING) * (2 * RING) + (zz % RING) * 2 + cc, yy)

    partner = at(x, z, 1 - c)
    prim = (x, z)
    seco = (z, x)

    def hop(axis, direction):
        step = 1 if direction == 0 else RING - 1
        return at(x + step, z) if axis == 0 else at(x, z + step)

    def load_acts(e, slot):
        return pltpu.make_async_copy(acts.at[pl.ds(e * SEQ, SEQ), :], abuf.at[slot], abuf_sem.at[slot])

    def load_grads(e):
        rows = pl.ds(e * SEQ, SEQ)
        return pltpu.make_async_copy(grads.at[rows, :], graw.at[c, rows, :], grad_sem.at[e])

    load_acts(0, 0).start()
    load_grads(0).start()
    load_acts(1, 1).start()
    for e in range(1, examples):
        load_grads(e).start()

    peers = [hop(a, d) for a in (0, 1) for d in (0, 1)]
    me8 = c * 4 + y
    group = []
    for d in range(1, 8):
        other = (me8 + d) % 8
        group.append((other, at(x, z, other // 4, other % 4)))
    barrier = pltpu.get_barrier_semaphore()
    for device in peers + [g[1] for g in group]:
        pl.semaphore_signal(barrier, inc=1, device_id=device, device_id_type=MESH)
    pl.semaphore_wait(barrier, 11)

    mine = pl.ds(pl.multiple_of(c * tokens, tokens), tokens)
    send_grads = pltpu.make_async_remote_copy(
        src_ref=grads, dst_ref=graw.at[c], send_sem=xs_grads, recv_sem=xr_grads,
        device_id=partner, device_id_type=MESH)
    send_grads.start()

    def column_block(j, core):
        return pl.ds(pl.multiple_of(j * 256 + core * 128, 128), 128)

    def send_column(j):
        return pltpu.make_async_remote_copy(
            src_ref=acts.at[:, column_block(j, 1 - c)], dst_ref=acts_c.at[j, mine, :],
            send_sem=xs_acts.at[j], recv_sem=xr_acts.at[j], device_id=partner, device_id_type=MESH)

    def load_column(j):
        return pltpu.make_async_copy(acts.at[:, column_block(j, c)], acts_c.at[j, mine, :], col_sem.at[j])

    for j in range(blocks):
        send_column(j).start()
    for j in range(blocks):
        load_column(j).start()

    for e in range(examples):
        slot = e % 2
        load_acts(e, slot).wait()
        load_grads(e).wait()
        low, high = pl.ds(0, 256), pl.ds(256, 256)
        a_all = abuf[slot]
        b_rows = pl.ds(e * SEQ, SEQ)
        b_all = graw[c, b_rows, :]
        b_low = graw[c, pl.ds(e * SEQ, 256), :]
        b_high = graw[c, pl.ds(e * SEQ + 256, 256), :]
        ga = lax.dot_general(a_all, abuf[slot, low, :], CONTRACT_LAST, preferred_element_type=F32)
        gb = lax.dot_general(b_all, b_low, CONTRACT_LAST, preferred_element_type=F32)
        both = ga * gb
        total = fold(both[:256]) + 2.0 * fold(both[256:])
        a_high = abuf[slot, high, :]
        ga = lax.dot_general(a_high, a_high, CONTRACT_LAST, preferred_element_type=F32)
        gb = lax.dot_general(b_high, b_high, CONTRACT_LAST, preferred_element_type=F32)
        norm_own[e] = total + fold(ga * gb)
        if e + 2 < examples:
            load_acts(e + 2, slot).start()
        columns = pl.ds(pl.multiple_of(c * tokens + e * SEQ, SEQ), SEQ)
        g_t[:, columns] = b_all.T

    def send_norms(other, device):
        return pltpu.make_async_remote_copy(
            src_ref=norm_own, dst_ref=norm_all.at[me8], send_sem=ns_sem.at[other],
            recv_sem=nr_sem.at[me8], device_id=device, device_id_type=MESH)

    for other, device in group:
        send_norms(other, device).start()

    send_grads.wait_recv()
    theirs = 1 - c
    for e in range(examples):
        columns = pl.ds(pl.multiple_of(theirs * tokens + e * SEQ, SEQ), SEQ)
        g_t[:, columns] = graw[theirs, pl.ds(e * SEQ, SEQ), :].T

    norm_all[me8] = norm_own[...]
    for other, device in group:
        pltpu.make_async_remote_copy(
            src_ref=norm_own, dst_ref=norm_all.at[other], send_sem=ns_sem.at[other],
            recv_sem=nr_sem.at[other], device_id=device, device_id_type=MESH).wait_recv()

    limit = bound[0]
    factors = []
    for core in range(2):
        summed = norm_all[4 * core] + norm_all[4 * core + 1] + norm_all[4 * core + 2] + norm_all[4 * core + 3]
        for e in range(examples):
            norm_sq = jnp.sum(summed[e], axis=(0, 1), keepdims=True)
            clip = jnp.minimum(1.0, limit / jnp.sqrt(norm_sq + 1e-06))
            factors.append(clip / limit)

    def scale(a):
        for e, factor in enumerate(factors):
            rows, columns = pl.ds(a * half_cols, half_cols), pl.ds(e * SEQ, SEQ)
            g_t[rows, columns] = (g_t[rows, columns].astype(F32) * factor).astype(BF16)

    roles = (2, 1, 3, 0)

    def chunk(a, step):
        goal = (prim[a] + step) % RING
        parts = []
        for k in range(RING):
            side = (seco[a] + roles[k]) % RING
            parts.append(acts_c[goal * RING + side if a == 0 else side * RING + goal])
        return jnp.dot(g_t[pl.ds(a * half_cols, half_cols), :], jnp.concatenate(parts, axis=1),
                       preferred_element_type=F32)

    def cut(product, half, k):
        return product[half * 256:(half + 1) * 256, k * 128:(k + 1) * 128]

    def opp_copy(a, d):
        return pltpu.make_async_remote_copy(
            src_ref=s_opp.at[a, d], dst_ref=r_opp.at[a, d], send_sem=s1_opp.at[a, d],
            recv_sem=r1_opp.at[a, d], device_id=hop(a, d), device_id_type=MESH)

    def fin_copy(a, d, half, k):
        return pltpu.make_async_remote_copy(
            src_ref=s_nb.at[a, d, half, k], dst_ref=r_fin.at[a, d, half, k], send_sem=s1_fin.at[a, d, half, k],
            recv_sem=r1_fin.at[a, d, half, k], device_id=hop(a, d), device_id_type=MESH)

    def do_opp(a):
        product = chunk(a, 2)
        for d in (0, 1):
            for k in range(RING):
                s_opp[a, d, k] = cut(product, d, k).astype(BF16)
            opp_copy(a, d).start()

    def do_neighbour(a, d):
        product = chunk(a, 1 if d == 0 else 3)
        plain = 1 - d
        for k in range(RING):
            s_nb[a, d, plain, k] = cut(product, plain, k).astype(BF16)
            fin_copy(a, d, plain, k).start()
            hold[a, d, k] = cut(product, d, k)

    def do_pass(a, d):
        opp_copy(a, d).wait_recv()
        for k in range(RING):
            s_nb[a, d, d, k] = (hold[a, d, k] + r_opp[a, d, k].astype(F32)).astype(BF16)
            fin_copy(a, d, d, k).start()

    def do_own(a):
        product = chunk(a, 0)
        for half in (0, 1):
            for k in range(RING):
                own[a, half, k] = cut(product, half, k)

    for j in range(blocks):
        load_column(j).wait()
        send_column(j).wait_recv()
    scale(0)
    do_opp(0)
    scale(1)
    do_opp(1)
    do_neighbour(0, 0)
    do_neighbour(0, 1)
    do_neighbour(1, 0)
    do_pass(0, 0)
    do_pass(0, 1)
    do_neighbour(1, 1)
    do_pass(1, 0)
    do_pass(1, 1)
    do_own(0)
    do_own(1)

    def opp2_copy(a, d):
        return pltpu.make_async_remote_copy(
            src_ref=own.at[a, d, 0], dst_ref=r2_opp.at[a, d], send_sem=s2_opp.at[a, d],
            recv_sem=r2o_sem.at[a, d], device_id=hop(1 - a, d), device_id_type=MESH)

    def plain2_copy(a, d):
        return pltpu.make_async_remote_copy(
            src_ref=own.at[a, 1 - d, 1 + d], dst_ref=r2_fin.at[a, d, 1 - d], send_sem=s2_fin.at[a, d, 1 - d],
            recv_sem=r2f_sem.at[a, d, 1 - d], device_id=hop(1 - a, d), device_id_type=MESH)

    def pass2_copy(a, d):
        return pltpu.make_async_remote_copy(
            src_ref=s2.at[a, d], dst_ref=r2_fin.at[a, d, d], send_sem=s2_fin.at[a, d, d],
            recv_sem=r2f_sem.at[a, d, d], device_id=hop(1 - a, d), device_id_type=MESH)

    for k in range(RING):
        for a in (0, 1):
            for half in (0, 1):
                fin_copy(a, 0, half, k).wait_recv()
                fin_copy(a, 1, half, k).wait_recv()
                own[a, half, k] = own[a, half, k] + r_fin[a, 0, half, k].astype(F32) + r_fin[a, 1, half, k].astype(F32)
            if k == 0:
                opp2_copy(a, 0).start()
                opp2_copy(a, 1).start()
            elif k < 3:
                plain2_copy(a, k - 1).start()
    for a in (0, 1):
        for d in (0, 1):
            opp2_copy(a, d).wait_recv()
            s2[a, d] = own[a, d, 1 + d] + r2_opp[a, d]
            pass2_copy(a, d).start()
    for a in (0, 1):
        for half in (0, 1):
            for d in (0, 1):
                (pass2_copy if d == half else plain2_copy)(a, d).wait_recv()
            done = own[a, half, 3] + r2_fin[a, 0, half] + r2_fin[a, 1, half]
            out[:, pl.ds(a * half_cols + half * 256, 256)] = done.T

    send_grads.wait_send()
    for j in range(blocks):
        send_column(j).wait_send()
    for other, device in group:
        send_norms(other, device).wait_send()
    for a in (0, 1):
        for d in (0, 1):
            opp_copy(a, d).wait_send()
            for half in (0, 1):
                for k in range(RING):
                    fin_copy(a, d, half, k).wait_send()
            opp2_copy(a, d).wait_send()
            plain2_copy(a, d).wait_send()
            pass2_copy(a, d).wait_send()


def on_device(acts, out_grads, clip_bound, noise):
    tokens, width = acts.shape[1:]
    columns = out_grads.shape[2]
    rows = width // lax.axis_size("dp")
    examples = tokens // SEQ
    batch_total = examples * lax.axis_size("dp")
    out_factor = width / math.sqrt(batch_total)
    dma = pltpu.SemaphoreType.DMA
    summed = pl.pallas_call(
        kernel,
        out_shape=jax.ShapeDtypeStruct((rows, columns), F32),
        in_specs=[
            pl.BlockSpec(memory_space=pl.ANY),
            pl.BlockSpec(memory_space=pl.ANY),
            pl.BlockSpec(memory_space=pltpu.SMEM),
        ],
        out_specs=pl.BlockSpec(memory_space=pltpu.VMEM),
        scratch_shapes=[
            pltpu.VMEM((2, SEQ, width), BF16),
            pltpu.VMEM((2, tokens, columns), BF16),
            pltpu.VMEM((width // 256, 2 * tokens, 128), BF16),
            pltpu.VMEM((columns, 2 * tokens), BF16),
            pltpu.VMEM((examples, 8, 128), F32),
            pltpu.VMEM((8, examples, 8, 128), F32),
            pltpu.VMEM((2, 2, RING, 256, 128), BF16),
            pltpu.VMEM((2, 2, 2, RING, 256, 128), BF16),
            pltpu.VMEM((2, 2, RING, 256, 128), F32),
            pltpu.VMEM((2, 2, RING, 256, 128), BF16),
            pltpu.VMEM((2, 2, 2, RING, 256, 128), BF16),
            pltpu.VMEM((2, 2, RING, 256, 128), F32),
            pltpu.VMEM((2, 2, 256, 128), F32),
            pltpu.VMEM((2, 2, 256, 128), F32),
            pltpu.VMEM((2, 2, 2, 256, 128), F32),
            dma((2,)),
            dma((examples,)),
            dma((width // 256,)),
            dma((width // 256,)),
            dma((width // 256,)),
            dma,
            dma,
            dma((8,)),
            dma((8,)),
            dma((2, 2)),
            dma((2, 2)),
            dma((2, 2, 2, RING)),
            dma((2, 2, 2, RING)),
            dma((2, 2)),
            dma((2, 2)),
            dma((2, 2, 2)),
            dma((2, 2, 2)),
        ],
        compiler_params=pltpu.CompilerParams(
            collective_id=0, has_side_effects=True, vmem_limit_bytes=63 * 2**20
        ),
    )(acts[0], out_grads[0], clip_bound)
    return (summed * out_factor + noise[0])[None]


def solution(mesh):
    placed = (P(None, "dp", None), P(None, "dp", "mp"), P(), P(None, "dp", "mp"))
    return jax.shard_map(
        on_device, mesh=mesh, in_specs=placed, out_specs=P(None, "dp", "mp"), check_vma=False
    )
```

time: 191 us -> 65.9 us (0.35)
  waiting for transfers between devices: 119 us -> 0 us
  Pallas kernels: 0 us -> 63.1 us
  matrix products: 48.9 us -> 0 us
  between operations: 14.1 us -> 0.73 us
  starting transfers between devices: 4.58 us -> 0 us
  local copies, waits for them, and re-layouts: 2.87 us -> 0.01 us
    reduce_scatter x1 -> x0, waiting for transfers between devices: 115 us -> none  [on_device(): lax.psum_scatter(term_rows(jnp.int32(0), model_width // lax.axis_size('dp...]
    pallas_call x0 -> x1, Pallas kernels: none -> 63.1 us  [on_device(): pl.pallas_call(kernel, out_shape=jax.ShapeDtypeStruct((rows, columns), F3...]
    dot_general x3 -> x0, matrix products: 48.9 us -> none  [the longest x1 24.2 us: term_rows(): lax.dot_general(act_block, scaled, (((0,), (0,)), ((), ())), preferred_el...]
    all_to_all x1 -> x0, starting transfers between devices: 4.57 us -> none  [sent_to_all(): lax.all_to_all(jnp.broadcast_to(array[None], (devices, *array.shape)), ax...]
    all_to_all x1 -> x0, waiting for transfers between devices: 4.55 us -> none  [sent_to_all(): lax.all_to_all(jnp.broadcast_to(array[None], (devices, *array.shape)), ax...]
  transfers between devices with their start and end apart: 2 -> 0, of which waited for: 2 -> 0; matrix products, arithmetic and copies ran while one was open for 0% -> 0% of each run, Pallas kernels for 0% -> 0%
where the time goes in v1:
time: 65.9 us; the launch traced here: 65.8 us
  Pallas kernels  63.1 us (96%)
  other arithmetic  1.91 us (3%)
  between operations  0.73 us (1%)
    pallas_call x1, Pallas kernels, on_device(): pl.pallas_call(kernel, out_shape=jax.ShapeDtypeStruct((rows, columns), F3...  63.1 us
    broadcast_in_dim x1, other arithmetic, on_device(): return (summed * out_factor + noise[0])[None]  1.91 us

profile of v1, /device:TPU:0, one launch (start us, length us, event | category | flops | bytes accessed | tf_op | source)
XLA Modules:
  0.0 65.8 jit_solution(1484462635391060226)
XLA Ops:
  0.0 0.0 copy-start
  0.7 63.1 %shard_map.46 = f32[128,1024]{1,0:T(8,128)} custom-call(bf16[2048,4096]{1,0:T(8,128)(2,1)} %bitcast.8, bf16[2048,1024]{1,0:T(8,128)(2,1)} %bitcast.9, f32[1]{0:T(128)S(6)} %copy.5.bound), custom_call_target="tpu_custom_call" | custom-call | tf_op jit(solution)/shard_map/pallas_call | solution.py:280
  63.8 0.0 copy-done
  63.8 1.9 %fusion = f32[1,128,1024]{2,1,0:T(8,128)} fusion(f32[1,128,1024]{2,1,0:T(8,128)S(1)} %copy-done, f32[128,1024]{1,0:T(8,128)} %shard_map.46), kind=kLoop, calls=%fused_computation.1 | loop fusion | flops 262144 | bytes 1572864 | tf_op jit(solution)/shard_map/broadcast_in_dim | solution.py:327
Async XLA Ops:
  0.0 63.8 %copy-start = (f32[1,128,1024]{2,1,0:T(8,128)S(1)}, f32[1,128,1024]{2,1,0:T(8,128)}, u32[]{:S(2)}) copy-start(f32[1,128,1024]{2,1,0:T(8,128)} %param.7) | copy-start | bytes 1572868

commit v2 on v1

v2 whole, which is shorter than its diff:
```python
import math

import jax
import jax.numpy as jnp
from jax import lax
from jax.experimental import pallas as pl
from jax.experimental.pallas import tpu as pltpu
from jax.sharding import PartitionSpec as P

SEQ = 512
RING = 4
MESH = pl.DeviceIdType.MESH
F32 = jnp.float32
BF16 = jnp.bfloat16
CONTRACT_LAST = (((1,), (1,)), ((), ()))


def fold(product):
    rows, cols = product.shape
    return jnp.sum(product.reshape(rows // 8, 8, cols // 128, 128), axis=(0, 2))


def kernel(acts, grads, bound, out, abuf, graw, acts_c, g_t, ahead, norm_own, norm_all,
           s_opp, s_nb, r_opp, r_fin, own, r2_opp, s2, r2_fin,
           abuf_sem, grad_sem, col_sem, xs_acts, xr_acts, xs_grads, xr_grads, ns_sem, nr_sem,
           s1_opp, r1_opp, s1_fin, r1_fin, s2_opp, r2o_sem, s2_fin, r2f_sem):
    dp = lax.axis_index("dp")
    y = lax.axis_index("mp")
    x, z, c = dp // (2 * RING), (dp // 2) % RING, dp % 2
    tokens = acts.shape[0]
    examples = tokens // SEQ
    blocks = acts.shape[1] // 256
    half_cols = grads.shape[1] // 2

    def at(xx, zz, cc=c, yy=y):
        return ((xx % RING) * (2 * RING) + (zz % RING) * 2 + cc, yy)

    partner = at(x, z, 1 - c)
    prim = (x, z)
    seco = (z, x)

    def hop(axis, direction):
        step = 1 if direction == 0 else RING - 1
        return at(x + step, z) if axis == 0 else at(x, z + step)

    roles = (2, 1, 3, 0)

    def load_acts(e, slot):
        return pltpu.make_async_copy(acts.at[pl.ds(e * SEQ, SEQ), :], abuf.at[slot], abuf_sem.at[slot])

    def load_grads(e):
        rows = pl.ds(e * SEQ, SEQ)
        return pltpu.make_async_copy(grads.at[rows, :], graw.at[c, rows, :], grad_sem.at[e])

    load_grads(0).start()
    load_acts(0, 0).start()

    peers = [hop(a, d) for a in (0, 1) for d in (0, 1)]
    me8 = c * 4 + y
    group = []
    for d in range(1, 8):
        other = (me8 + d) % 8
        group.append((other, at(x, z, other // 4, other % 4)))
    barrier = pltpu.get_barrier_semaphore()
    for device in peers + [g[1] for g in group]:
        pl.semaphore_signal(barrier, inc=1, device_id=device, device_id_type=MESH)
    mine = pl.ds(pl.multiple_of(c * tokens, tokens), tokens)
    send_grads = pltpu.make_async_remote_copy(
        src_ref=grads, dst_ref=graw.at[c], send_sem=xs_grads, recv_sem=xr_grads,
        device_id=partner, device_id_type=MESH)

    order = []
    for first in [(2, None), (None, 2), (1, None), (3, None), (None, 1), (None, 3), (0, None)]:
        for step in roles:
            pair = (first[0] if first[0] is not None else step, first[1] if first[1] is not None else step)
            if pair not in order:
                order.append(pair)

    def block(i):
        dx, dz = order[i]
        return ((x + dx) % RING) * RING + (z + dz) % RING

    def column_block(j, core):
        return pl.ds(pl.multiple_of(j * 256 + core * 128, 128), 128)

    def send_column(i):
        j = block(i)
        return pltpu.make_async_remote_copy(
            src_ref=acts.at[:, column_block(j, 1 - c)], dst_ref=acts_c.at[j, mine, :],
            send_sem=xs_acts.at[i], recv_sem=xr_acts.at[i], device_id=partner, device_id_type=MESH)

    def load_column(i):
        j = block(i)
        return pltpu.make_async_copy(acts.at[:, column_block(j, c)], acts_c.at[j, mine, :], col_sem.at[i])

    def do_gram(e):
        slot = e % 2
        load_grads(e).wait()
        load_acts(e, slot).wait()
        if e + 1 < examples:
            load_grads(e + 1).start()
        if e == 0:
            load_acts(1, 1).start()
        b_all = graw[c, pl.ds(e * SEQ, SEQ), :]
        b_low = graw[c, pl.ds(e * SEQ, 256), :]
        b_high = graw[c, pl.ds(e * SEQ + 256, 256), :]
        ga = lax.dot_general(abuf[slot], abuf[slot, pl.ds(0, 256), :], CONTRACT_LAST, preferred_element_type=F32)
        gb = lax.dot_general(b_all, b_low, CONTRACT_LAST, preferred_element_type=F32)
        both = ga * gb
        total = fold(both[:256]) + 2.0 * fold(both[256:])
        a_high = abuf[slot, pl.ds(256, 256), :]
        ga = lax.dot_general(a_high, a_high, CONTRACT_LAST, preferred_element_type=F32)
        gb = lax.dot_general(b_high, b_high, CONTRACT_LAST, preferred_element_type=F32)
        norm_own[e] = total + fold(ga * gb)
        if e + 2 < examples:
            load_acts(e + 2, slot).start()
        columns = pl.ds(pl.multiple_of(c * tokens + e * SEQ, SEQ), SEQ)
        g_t[:, columns] = b_all.T

    early = 4
    do_gram(0)
    pl.semaphore_wait(barrier, 11)
    send_grads.start()
    for i in range(early):
        send_column(i).start()
    for e in range(1, examples):
        do_gram(e)
        for i in range((e - 1) * 4, blocks if e + 1 == examples else e * 4):
            load_column(i).start()

    def send_norms(other, device):
        return pltpu.make_async_remote_copy(
            src_ref=norm_own, dst_ref=norm_all.at[me8], send_sem=ns_sem.at[other],
            recv_sem=nr_sem.at[me8], device_id=device, device_id_type=MESH)

    for other, device in group:
        send_norms(other, device).start()
    for i in range(early, blocks):
        send_column(i).start()

    def do_theirs():
        send_grads.wait_recv()
        theirs = 1 - c
        for e in range(examples):
            columns = pl.ds(pl.multiple_of(theirs * tokens + e * SEQ, SEQ), SEQ)
            g_t[:, columns] = graw[theirs, pl.ds(e * SEQ, SEQ), :].T

    do_theirs()

    arrived = set()

    def chunk_blocks(a, step):
        indices = [order.index((step, role) if a == 0 else (role, step)) for role in roles]
        for i in indices:
            if i not in arrived:
                arrived.add(i)
                load_column(i).wait()
                send_column(i).wait_recv()
        return [block(i) for i in indices]

    def chunk(a, step, half):
        right = jnp.concatenate([acts_c[j] for j in chunk_blocks(a, step)], axis=1)
        return jnp.dot(g_t[pl.ds(a * half_cols + half * 256, 256), :], right, preferred_element_type=F32)

    def cut(product, k):
        return product[:, k * 128:(k + 1) * 128]

    def do_ahead(half):
        places = chunk_blocks(0, 2)
        for e in range(2 * examples):
            span = pl.ds(e * SEQ, SEQ)
            right = jnp.concatenate([acts_c[j, span, :] for j in places], axis=1)
            ahead[half, e] = jnp.dot(g_t[pl.ds(half * 256, 256), span], right, preferred_element_type=F32)

    do_ahead(0)
    do_ahead(1)

    def do_norm_wait():
        norm_all[me8] = norm_own[...]
        for other, device in group:
            pltpu.make_async_remote_copy(
                src_ref=norm_own, dst_ref=norm_all.at[other], send_sem=ns_sem.at[other],
                recv_sem=nr_sem.at[other], device_id=device, device_id_type=MESH).wait_recv()

    do_norm_wait()

    limit = bound[0]
    factors = []
    for core in range(2):
        summed = norm_all[4 * core] + norm_all[4 * core + 1] + norm_all[4 * core + 2] + norm_all[4 * core + 3]
        for e in range(examples):
            norm_sq = jnp.sum(summed[e], axis=(0, 1), keepdims=True)
            clip = jnp.minimum(1.0, limit / jnp.sqrt(norm_sq + 1e-06))
            factors.append(clip / limit)

    def do_scale(a, half):
        for e, factor in enumerate(factors):
            rows, columns = pl.ds(a * half_cols + half * 256, 256), pl.ds(e * SEQ, SEQ)
            g_t[rows, columns] = (g_t[rows, columns].astype(F32) * factor).astype(BF16)

    def opp_copy(a, d):
        return pltpu.make_async_remote_copy(
            src_ref=s_opp.at[a, d], dst_ref=r_opp.at[a, d], send_sem=s1_opp.at[a, d],
            recv_sem=r1_opp.at[a, d], device_id=hop(a, d), device_id_type=MESH)

    def fin_copy(a, d, half, k):
        return pltpu.make_async_remote_copy(
            src_ref=s_nb.at[a, d, half, k], dst_ref=r_fin.at[a, d, half, k], send_sem=s1_fin.at[a, d, half, k],
            recv_sem=r1_fin.at[a, d, half, k], device_id=hop(a, d), device_id_type=MESH)

    def do_opp(a, d):
        if a == 0:
            product = ahead[d, 0] * factors[0]
            for e in range(1, 2 * examples):
                product = product + ahead[d, e] * factors[e]
        else:
            product = chunk(a, 2, d)
        for k in range(RING):
            s_opp[a, d, k] = cut(product, k).astype(BF16)
        opp_copy(a, d).start()

    def do_plain(a, d):
        product = chunk(a, 1 if d == 0 else 3, 1 - d)
        for k in range(RING):
            s_nb[a, d, 1 - d, k] = cut(product, k).astype(BF16)
            fin_copy(a, d, 1 - d, k).start()

    def do_pass(a, d):
        product = chunk(a, 1 if d == 0 else 3, d)
        opp_copy(a, d).wait_recv()
        for k in range(RING):
            s_nb[a, d, d, k] = (cut(product, k) + r_opp[a, d, k].astype(F32)).astype(BF16)
            fin_copy(a, d, d, k).start()

    def do_own(a, half):
        product = chunk(a, 0, half)
        for k in range(RING):
            own[a, half, k] = cut(product, k)

    pairs = [(a, d) for a in (0, 1) for d in (0, 1)]
    do_opp(0, 0)
    do_opp(0, 1)
    for d in (0, 1):
        do_scale(1, d)
        do_opp(1, d)
    for a, d in pairs:
        if a == 0:
            do_scale(0, 1 - d)
        do_plain(a, d)
    for a, d in pairs:
        do_pass(a, d)
    do_own(0, 0)
    do_own(0, 1)

    def opp2_copy(a, d):
        return pltpu.make_async_remote_copy(
            src_ref=own.at[a, d, 0], dst_ref=r2_opp.at[a, d], send_sem=s2_opp.at[a, d],
            recv_sem=r2o_sem.at[a, d], device_id=hop(1 - a, d), device_id_type=MESH)

    def plain2_copy(a, d):
        return pltpu.make_async_remote_copy(
            src_ref=own.at[a, 1 - d, 1 + d], dst_ref=r2_fin.at[a, d, 1 - d], send_sem=s2_fin.at[a, d, 1 - d],
            recv_sem=r2f_sem.at[a, d, 1 - d], device_id=hop(1 - a, d), device_id_type=MESH)

    def pass2_copy(a, d):
        return pltpu.make_async_remote_copy(
            src_ref=s2.at[a, d], dst_ref=r2_fin.at[a, d, d], send_sem=s2_fin.at[a, d, d],
            recv_sem=r2f_sem.at[a, d, d], device_id=hop(1 - a, d), device_id_type=MESH)

    def do_join(a, k):
        for half in (0, 1):
            fin_copy(a, 0, half, k).wait_recv()
            fin_copy(a, 1, half, k).wait_recv()
            own[a, half, k] = own[a, half, k] + r_fin[a, 0, half, k].astype(F32) + r_fin[a, 1, half, k].astype(F32)
        if k == 0:
            opp2_copy(a, 0).start()
            opp2_copy(a, 1).start()
        elif k < 3:
            plain2_copy(a, k - 1).start()

    def do_pass2(a, d):
        opp2_copy(a, d).wait_recv()
        s2[a, d] = own[a, d, 1 + d] + r2_opp[a, d]
        pass2_copy(a, d).start()

    def do_finish(a, half):
        for d in (0, 1):
            (pass2_copy if d == half else plain2_copy)(a, d).wait_recv()
        done = own[a, half, 3] + r2_fin[a, 0, half] + r2_fin[a, 1, half]
        out[:, pl.ds(a * half_cols + half * 256, 256)] = done.T

    do_join(0, 0)
    do_own(1, 0)
    do_own(1, 1)
    do_join(1, 0)
    for k in range(1, RING):
        do_join(0, k)
        do_join(1, k)
    for a in (0, 1):
        for d in (0, 1):
            do_pass2(a, d)
    for a in (0, 1):
        for half in (0, 1):
            do_finish(a, half)

    send_grads.wait_send()
    for i in range(blocks):
        send_column(i).wait_send()
    for other, device in group:
        send_norms(other, device).wait_send()
    for a in (0, 1):
        for d in (0, 1):
            opp_copy(a, d).wait_send()
            for half in (0, 1):
                for k in range(RING):
                    fin_copy(a, d, half, k).wait_send()
            opp2_copy(a, d).wait_send()
            plain2_copy(a, d).wait_send()
            pass2_copy(a, d).wait_send()


def on_device(acts, out_grads, clip_bound, noise):
    tokens, width = acts.shape[1:]
    columns = out_grads.shape[2]
    rows = width // lax.axis_size("dp")
    examples = tokens // SEQ
    batch_total = examples * lax.axis_size("dp")
    out_factor = width / math.sqrt(batch_total)
    dma = pltpu.SemaphoreType.DMA
    summed = pl.pallas_call(
        kernel,
        out_shape=jax.ShapeDtypeStruct((rows, columns), F32),
        in_specs=[
            pl.BlockSpec(memory_space=pl.ANY),
            pl.BlockSpec(memory_space=pl.ANY),
            pl.BlockSpec(memory_space=pltpu.SMEM),
        ],
        out_specs=pl.BlockSpec(memory_space=pltpu.VMEM),
        scratch_shapes=[
            pltpu.VMEM((2, SEQ, width), BF16),
            pltpu.VMEM((2, tokens, columns), BF16),
            pltpu.VMEM((width // 256, 2 * tokens, 128), BF16),
            pltpu.VMEM((columns, 2 * tokens), BF16),
            pltpu.VMEM((2, 2 * examples, 256, RING * 128), F32),
            pltpu.VMEM((examples, 8, 128), F32),
            pltpu.VMEM((8, examples, 8, 128), F32),
            pltpu.VMEM((2, 2, RING, 256, 128), BF16),
            pltpu.VMEM((2, 2, 2, RING, 256, 128), BF16),
            pltpu.VMEM((2, 2, RING, 256, 128), BF16),
            pltpu.VMEM((2, 2, 2, RING, 256, 128), BF16),
            pltpu.VMEM((2, 2, RING, 256, 128), F32),
            pltpu.VMEM((2, 2, 256, 128), F32),
            pltpu.VMEM((2, 2, 256, 128), F32),
            pltpu.VMEM((2, 2, 2, 256, 128), F32),
            dma((2,)),
            dma((examples,)),
            dma((width // 256,)),
            dma((width // 256,)),
            dma((width // 256,)),
            dma,
            dma,
            dma((8,)),
            dma((8,)),
            dma((2, 2)),
            dma((2, 2)),
            dma((2, 2, 2, RING)),
            dma((2, 2, 2, RING)),
            dma((2, 2)),
            dma((2, 2)),
            dma((2, 2, 2)),
            dma((2, 2, 2)),
        ],
        compiler_params=pltpu.CompilerParams(
            collective_id=0, has_side_effects=True, vmem_limit_bytes=63 * 2**20
        ),
    )(acts[0], out_grads[0], clip_bound)
    return (summed * out_factor + noise[0])[None]


def solution(mesh):
    placed = (P(None, "dp", None), P(None, "dp", "mp"), P(), P(None, "dp", "mp"))
    return jax.shard_map(
        on_device, mesh=mesh, in_specs=placed, out_specs=P(None, "dp", "mp"), check_vma=False
    )
```

time: 65.9 us -> 58.6 us (0.89)
  Pallas kernels: 63.1 us -> 55.8 us
    pallas_call x1, Pallas kernels: 63.1 us -> 55.8 us  [on_device(): pl.pallas_call(kernel, out_shape=jax.ShapeDtypeStruct((rows, columns), F3...]
where the time goes in v2:
time: 58.6 us; the launch traced here: 58.4 us
  Pallas kernels  55.8 us (95%)
  other arithmetic  1.91 us (3%)
  between operations  0.73 us (1%)
    pallas_call x1, Pallas kernels, on_device(): pl.pallas_call(kernel, out_shape=jax.ShapeDtypeStruct((rows, columns), F3...  55.8 us
    broadcast_in_dim x1, other arithmetic, on_device(): return (summed * out_factor + noise[0])[None]  1.91 us

profile of v2, /device:TPU:0, one launch (start us, length us, event | category | flops | bytes accessed | tf_op | source)
XLA Modules:
  0.0 58.4 jit_solution(17035756892912914123)
XLA Ops:
  0.0 0.0 copy-start
  0.7 55.8 %shard_map.46 = f32[128,1024]{1,0:T(8,128)} custom-call(bf16[2048,4096]{1,0:T(8,128)(2,1)} %bitcast.8, bf16[2048,1024]{1,0:T(8,128)(2,1)} %bitcast.9, f32[1]{0:T(128)S(6)} %copy.5.bound), custom_call_target="tpu_custom_call" | custom-call | tf_op jit(solution)/shard_map/pallas_call | solution.py:330
  56.5 0.0 copy-done
  56.5 1.9 %fusion = f32[1,128,1024]{2,1,0:T(8,128)} fusion(f32[1,128,1024]{2,1,0:T(8,128)S(1)} %copy-done, f32[128,1024]{1,0:T(8,128)} %shard_map.46), kind=kLoop, calls=%fused_computation.1 | loop fusion | flops 262144 | bytes 1572864 | tf_op jit(solution)/shard_map/broadcast_in_dim | solution.py:377
Async XLA Ops:
  0.0 56.5 %copy-start = (f32[1,128,1024]{2,1,0:T(8,128)S(1)}, f32[1,128,1024]{2,1,0:T(8,128)}, u32[]{:S(2)}) copy-start(f32[1,128,1024]{2,1,0:T(8,128)} %param.7) | copy-start | bytes 1572868

commit v3 on v2

--- a/solution.py
+++ b/solution.py
@@ -36,12 +36,14 @@
         return ((xx % RING) * (2 * RING) + (zz % RING) * 2 + cc, yy)
 
     partner = at(x, z, 1 - c)
-    prim = (x, z)
-    seco = (z, x)
+
+    def swapped(core, u, v):
+        return u + core * (v - u), v + core * (u - v)
 
     def hop(axis, direction):
         step = 1 if direction == 0 else RING - 1
-        return at(x + step, z) if axis == 0 else at(x, z + step)
+        dx, dz = swapped(c, step, 0) if axis == 0 else swapped(c, 0, step)
+        return at(x + dx, z + dz)
 
     roles = (2, 1, 3, 0)
 
@@ -76,21 +78,21 @@
             if pair not in order:
                 order.append(pair)
 
-    def block(i):
-        dx, dz = order[i]
+    def block(i, core):
+        dx, dz = swapped(core, *order[i])
         return ((x + dx) % RING) * RING + (z + dz) % RING
 
     def column_block(j, core):
         return pl.ds(pl.multiple_of(j * 256 + core * 128, 128), 128)
 
     def send_column(i):
-        j = block(i)
+        j = block(i, 1 - c)
         return pltpu.make_async_remote_copy(
             src_ref=acts.at[:, column_block(j, 1 - c)], dst_ref=acts_c.at[j, mine, :],
             send_sem=xs_acts.at[i], recv_sem=xr_acts.at[i], device_id=partner, device_id_type=MESH)
 
     def load_column(i):
-        j = block(i)
+        j = block(i, c)
         return pltpu.make_async_copy(acts.at[:, column_block(j, c)], acts_c.at[j, mine, :], col_sem.at[i])
 
     def do_gram(e):
@@ -156,7 +158,7 @@
                 arrived.add(i)
                 load_column(i).wait()
                 send_column(i).wait_recv()
-        return [block(i) for i in indices]
+        return [block(i, c) for i in indices]
 
     def chunk(a, step, half):
         right = jnp.concatenate([acts_c[j] for j in chunk_blocks(a, step)], axis=1)

time: 58.6 us -> 57.5 us (0.981); the launches traced: 58.4 us -> 56.4 us
  Pallas kernels: 55.8 us -> 53.8 us
    pallas_call x1, Pallas kernels: 55.8 us -> 53.8 us  [on_device(): pl.pallas_call(kernel, out_shape=jax.ShapeDtypeStruct((rows, columns), F3...]
where the time goes in v3:
time: 57.5 us; the launch traced here: 56.4 us
  Pallas kernels  53.8 us (94%)
  other arithmetic  1.91 us (3%)
  between operations  0.73 us (1%)
    pallas_call x1, Pallas kernels, on_device(): pl.pallas_call(kernel, out_shape=jax.ShapeDtypeStruct((rows, columns), F3...  53.8 us
    broadcast_in_dim x1, other arithmetic, on_device(): return (summed * out_factor + noise[0])[None]  1.91 us

profile of v3, /device:TPU:0, one launch (start us, length us, event | category | flops | bytes accessed | tf_op | source)
XLA Modules:
  0.0 56.4 jit_solution(14049425594163332284)
XLA Ops:
  0.0 0.0 copy-start
  0.7 53.8 %shard_map.46 = f32[128,1024]{1,0:T(8,128)} custom-call(bf16[2048,4096]{1,0:T(8,128)(2,1)} %bitcast.8, bf16[2048,1024]{1,0:T(8,128)(2,1)} %bitcast.9, f32[1]{0:T(128)S(6)} %copy.5.bound), custom_call_target="tpu_custom_call" | custom-call | tf_op jit(solution)/shard_map/pallas_call | solution.py:332
  54.5 0.0 copy-done
  54.5 1.9 %fusion = f32[1,128,1024]{2,1,0:T(8,128)} fusion(f32[1,128,1024]{2,1,0:T(8,128)S(1)} %copy-done, f32[128,1024]{1,0:T(8,128)} %shard_map.46), kind=kLoop, calls=%fused_computation.1 | loop fusion | flops 262144 | bytes 1572864 | tf_op jit(solution)/shard_map/broadcast_in_dim | solution.py:379
Async XLA Ops:
  0.0 54.5 %copy-start = (f32[1,128,1024]{2,1,0:T(8,128)S(1)}, f32[1,128,1024]{2,1,0:T(8,128)}, u32[]{:S(2)}) copy-start(f32[1,128,1024]{2,1,0:T(8,128)} %param.7) | copy-start | bytes 1572868
